TPU v7x, 128 devices: a whole 4x4x4 slice. The times are simulated.
128 devices in a mesh: psg: 16 (over x_hi, y, core), qry: 8 (over z, x_lo).
Axes of the slice: x: 4 (x_hi: 2, x_lo: 2; x = x_hi * 2 + x_lo), y: 4, z: 4, core: 2. Of those that a mesh axis runs over, the one named last changes fastest.
Arguments:
- hidden: bfloat16 [1024, 4096], P('qry'), may hold values from -6 to 6
- norm_gain: float32 [4096], replicated, may hold values from 0.5 to 1.5
- proj_weight: bfloat16 [4096, 4096], P('psg', 'qry'), may hold values from -0.09375 to 0.09375
- pq_codes: int32 [32768, 512], P('psg', 'qry'), may hold values from 0 to 255
- codebook: bfloat16 [512, 8, 256], P('qry'), may hold values from -560 to 560
- positives: int32 [1024], replicated, may hold values from 0 to 32767
Outputs:
- losses: float32 [1024], P('qry')
- hidden_grad: bfloat16 [1024, 4096], P('qry')
- weight_grad: float32 [4096, 4096], P('psg', 'qry')
- codebook_grad: float32 [512, 8, 256], P('qry')
All inputs are finite; a program needn't handle non-finite values.
Results may differ from a plain program's by a relative error of at most 0.019.
The roundings to bfloat16 on the way count: a program that leaves them out, or rounds other values in their place, can miss the bound.
Values may be sent and summed in bfloat16 or wider, within the bound.
A program may use at most 128 MiB of HBM per device.

v0:
```python
import jax
import jax.numpy as jnp
from jax import lax
from jax.sharding import Mesh
from jax.sharding import PartitionSpec as P

QRY = ("qry_0", "qry_1")
score_scale = 0.0625
norm_eps = 1e-06


def summed_rows(x, axes, dim):
    if not axes:
        return x
    nearer = lax.psum_scatter(x, axes[0], scatter_dimension=dim, tiled=True)
    return summed_rows(nearer, axes[1:], dim)


def sent_to_all(x, axis):
    copies = jnp.broadcast_to(x, (lax.axis_size(axis), *x.shape))
    return lax.all_to_all(copies, axis, split_axis=0, concat_axis=0, tiled=True)


def gathered_once(x, axis):
    leaves = jax.tree.leaves(x)
    turns = sorted(range(len(leaves)), key=lambda k: -leaves[k].size)
    width = (1, *leaves[turns[0]].shape)[-1]
    lines = [
        jnp.pad(leaves[k].reshape(-1), (0, -leaves[k].size % width)).reshape(-1, width)
        for k in turns
    ]
    both, at, found = (sent_to_all(jnp.concatenate(lines), axis), 0, {})
    for k, line in zip(turns, lines):
        piece = both[:, at : at + len(line)].reshape(len(both), -1)
        found[k] = piece[:, : leaves[k].size].reshape(-1, *leaves[k].shape)
        at += len(line)
    numbers = iter(range(len(leaves)))
    return jax.tree.map(lambda _: found[next(numbers)], x)


def folded_in_pairs(pieces, combine):
    while len(jax.tree.leaves(pieces)[0]) > 1:
        pieces = jax.vmap(combine)(
            *(jax.tree.map(lambda part: part[side::2], pieces) for side in (0, 1))
        )
    return jax.tree.map(lambda part: part[0], pieces)


def joined_all(x, axis, combine):
    pieces = gathered_once(x, axis)
    return folded_in_pairs(pieces, combine)


def code_hot(code_block, book):
    levels = lax.broadcasted_iota(jnp.int32, code_block.shape + (book.shape[2],), 2)
    return (code_block[:, :, None] == levels).astype(jnp.bfloat16)


def per_device(hidden, norm_gain, proj_weight, pq_codes, codebook, positives):
    gathered = lax.all_gather(hidden, QRY, axis=0, tiled=True)
    floats_all = gathered.astype(jnp.float32)
    inverse_all = lax.rsqrt(jnp.mean(floats_all * floats_all, axis=1, keepdims=True) + norm_eps)
    normed = (floats_all * inverse_all * norm_gain[None, :]).astype(jnp.bfloat16)
    columns = proj_weight.shape[1]
    whole_weight = lax.all_gather(proj_weight, "psg", axis=0, tiled=True)
    query_float = jnp.dot(normed, whole_weight, preferred_element_type=jnp.float32)
    queries = query_float.astype(jnp.bfloat16)
    passage_count = pq_codes.shape[0]
    sub_count = codebook.shape[0]
    sub_width = codebook.shape[1]
    block_rows = min(passage_count, 512)
    code_blocks = pq_codes.reshape(passage_count // block_rows, block_rows, sub_count)

    def decode(code_block):
        hot_table = code_hot(code_block, codebook)
        vectors = jnp.einsum(
            "pmk,mdk->pmd", hot_table, codebook, preferred_element_type=jnp.float32
        )
        return vectors.astype(jnp.bfloat16).reshape(block_rows, columns)

    passages = lax.map(decode, code_blocks).reshape(passage_count, columns)
    partial_value = (
        lax.dot_general(
            queries, passages, (((1,), (1,)), ((), ())), preferred_element_type=jnp.float32
        )
        * score_scale
    )
    qry_index = lax.axis_index(QRY)
    own_rows = hidden.shape[0]
    scores = summed_rows(partial_value, QRY, 0)
    row_targets = lax.dynamic_slice_in_dim(positives, qry_index * own_rows, own_rows, 0)
    local_target = row_targets - lax.axis_index("psg") * passage_count
    target = lax.broadcasted_iota(jnp.int32, scores.shape, 1) == local_target[:, None]
    local_max = jnp.max(scores, axis=1)
    positive_part = jnp.sum(jnp.where(target, scores, 0.0), axis=1)
    local_total = jnp.sum(jnp.exp(scores - local_max[:, None]), axis=1)

    def combine(first, second):
        higher = jnp.maximum(first[0], second[0])
        joined = first[1] * jnp.exp(first[0] - higher) + second[1] * jnp.exp(second[0] - higher)
        return (higher, joined, first[2] + second[2])

    row_max, row_total, positive_score = joined_all(
        (local_max, local_total, positive_part), "psg", combine
    )
    losses = jnp.log(row_total) + row_max - positive_score
    score_grad = (
        jnp.exp(scores - row_max[:, None]) / row_total[:, None] - target.astype(jnp.float32)
    ).astype(jnp.bfloat16)
    all_grad = lax.all_gather(score_grad, QRY, axis=0, tiled=True)
    query_part = jnp.dot(all_grad, passages, preferred_element_type=jnp.float32) * score_scale
    query_grad = lax.psum(query_part, "psg").astype(jnp.bfloat16)
    passage_grad = (
        lax.dot_general(
            all_grad, queries, (((0,), (0,)), ((), ())), preferred_element_type=jnp.float32
        )
        * score_scale
    ).astype(jnp.bfloat16)
    grad_blocks = passage_grad.reshape(
        passage_count // block_rows, block_rows, sub_count, sub_width
    )

    def add_book(carry, paired):
        code_block, grad_block = paired
        hot_table = code_hot(code_block, codebook)
        return (
            carry
            + jnp.einsum("pmk,pmd->mdk", hot_table, grad_block, preferred_element_type=jnp.float32),
            None,
        )

    book_part, unused = lax.scan(
        add_book, jnp.zeros(codebook.shape, jnp.float32), (code_blocks, grad_blocks)
    )
    codebook_grad = lax.psum(book_part.astype(jnp.bfloat16), "psg").astype(jnp.float32)
    row_span = proj_weight.shape[0]
    normed_rows = lax.dynamic_slice_in_dim(normed, lax.axis_index("psg") * row_span, row_span, 1)
    weight_grad = lax.dot_general(
        normed_rows, query_grad, (((0,), (0,)), ((), ())), preferred_element_type=jnp.float32
    )
    norm_part = lax.dot_general(
        query_grad, whole_weight, (((1,), (1,)), ((), ())), preferred_element_type=jnp.float32
    )
    norm_back = lax.psum_scatter(
        norm_part.astype(jnp.bfloat16), QRY, scatter_dimension=0, tiled=True
    ).astype(jnp.float32)
    floats_own = hidden.astype(jnp.float32)
    inverse_own = lax.rsqrt(jnp.mean(floats_own * floats_own, axis=1, keepdims=True) + norm_eps)
    scaled = norm_back * norm_gain[None, :]
    hidden_grad = (
        inverse_own * scaled
        - floats_own
        * inverse_own
        * inverse_own
        * inverse_own
        * jnp.mean(scaled * floats_own, axis=1, keepdims=True)
    ).astype(jnp.bfloat16)
    return (losses, hidden_grad, weight_grad, codebook_grad)


def solution(mesh):
    split = Mesh(mesh.devices.reshape(mesh.shape["psg"], 4, 2), ("psg", "qry_0", "qry_1"))
    return jax.shard_map(
        per_device,
        mesh=split,
        in_specs=(P(QRY, None), P(), P("psg", QRY), P("psg", QRY), P(QRY, None, None), P()),
        out_specs=(P(QRY), P(QRY, None), P("psg", QRY), P(QRY, None, None)),
        check_vma=False,
    )
```

profile of v0, /device:TPU:1, one launch (start us, length us, event | category | flops | bytes accessed | tf_op | source)
XLA Modules:
  0.0 852.5 jit_solution(15345686447529952865)
XLA Ops:
  7.2 0.7 all-gather.4.cloned.1.call-update
  7.9 0.7 all-gather.6.cloned.1.call-update
  8.7 1.1 copy.27
  9.8 33.1 %while.21 = (s32[]{:T(128)}, bf16[4,512,512]{2,1,0:T(8,128)(2,1)}, s32[4,512,64]{1,2,0:T(8,128)S(1)}, bf16[64,8,256]{2,1,0:T(8,128)(2,1)}, s32[]{:T(128)}) while((s32[]{:T(128)}, bf16[4,512,512]{2,1,0:T(8,128)(2,1)}, s32[4,512,64]{1,2,0:T(8,128)S(1)}, bf16[64,8,256]{2,1,0:T(8,128)(2,1)}, s32[]{:T(128)}) %tuple.74), condition=%wide.region_2.3_spmd, body=%wide.region_1.2_spmd.sunk | while | flops 142868480 | bytes 3277377 | solution.py:81
  9.8 7.2 fusion.43
  17.0 0.2 copy.29
  17.2 0.8 constant_dynamic-update-slice_fusion.2
  18.1 7.2 fusion.43
  25.5 0.9 constant_dynamic-update-slice_fusion.2
  26.4 7.2 fusion.43
  33.8 0.8 constant_dynamic-update-slice_fusion.2
  34.6 7.2 fusion.43
  42.0 0.9 constant_dynamic-update-slice_fusion.2
  42.9 138.0 %all-gather.4.cloned.1.call-done = bf16[1024,4096]{1,0:T(8,128)(2,1)} async-done(((bf16[128,4096]{1,0:T(8,128)(2,1)}), bf16[1024,4096]{1,0:T(8,128)(2,1)}) %all-gather.4.cloned.1.call-update) | async-done | bytes 8388624 | tf_op jit(solution)/shard_map/all_gather | solution.py:60
  180.9 5.1 fusion.10
  186.0 10.3 %fusion.12 = bf16[1024,4096]{1,0:T(8,128)(2,1)} fusion(bf16[1024,4096]{1,0:T(8,128)(2,1)} %all-gather.4.cloned.1.call-done, f32[4096]{0:T(1024)S(1)} %copy-done.1, f32[1024]{0:T(1024)S(1)} %add_rsqrt_fusion), kind=kLoop, calls=%fused_computation.19 | loop fusion | flops 16777216 | bytes 16797696 | tf_op jit(solution)/shard_map/convert_element_type | solution.py:63
  196.3 43.5 %all-gather.6.cloned.1.call-done = bf16[4096,512]{1,0:T(8,128)(2,1)} async-done(((bf16[256,512]{1,0:T(8,128)(2,1)}), bf16[4096,512]{1,0:T(8,128)(2,1)}) %all-gather.6.cloned.1.call-update) | async-done | bytes 4194320 | tf_op jit(solution)/shard_map/all_gather | solution.py:65
  239.8 9.1 %convolution_convert_fusion.1 = bf16[1024,512]{1,0:T(8,128)(2,1)S(1)} fusion(bf16[1024,4096]{1,0:T(8,128)(2,1)} %fusion.12, bf16[4096,512]{1,0:T(8,128)(2,1)} %all-gather.6.cloned.1.call-done), kind=kOutput, calls=%fused_computation.35 | convolution fusion | flops 4295491584 | bytes 13631488 | tf_op jit(solution)/shard_map/dot_general | solution.py:66
  248.9 1.0 copy-done.3
  249.8 5.6 convolution_multiply_fusion
  255.5 78.3 %reduce-scatter.4.cloned.1.call-done = f32[256,2048]{1,0:T(8,128)} async-done(((f32[1024,2048]{1,0:T(8,128)}), f32[256,2048]{1,0:T(8,128)}) %reduce-scatter.4.cloned.1.call-update) | async-done | bytes 2097168 | tf_op jit(solution)/shard_map/reduce_scatter | solution.py:15
  333.9 0.8 dynamic-slice_subtract_fusion
  334.6 35.3 %reduce-scatter.6.cloned.1.call-done = f32[128,2048]{1,0:T(8,128)} async-done(((f32[256,2048]{1,0:T(8,128)}), f32[128,2048]{1,0:T(8,128)}) %reduce-scatter.6.cloned.1.call-update) | async-done | bytes 1048592 | tf_op jit(solution)/shard_map/reduce_scatter | solution.py:15
  369.9 1.4 reduce_max.9
  371.3 1.6 exponential_reduce_fusion
  372.9 14.4 %all_to_all.5 = f32[16,3,128]{2,1,0:T(4,128)S(1)} all-to-all(f32[16,3,128]{2,1,0:T(4,128)S(1)} %broadcast_in_dim.28), channel_id=1, replica_groups=mesh['psg'=16,'qry_0'=4,'qry_1'=2] {'psg'}, dimensions={0} | all-to-all | bytes 49152 | tf_op jit(solution)/shard_map/all_to_all | solution.py:21
  387.7 0.5 bitcast_subtract_fusion
  388.3 2.4 subtract_convert_fusion
  390.8 87.4 %all-gather.8.cloned.1.call-done = bf16[1024,2048]{1,0:T(8,128)(2,1)} async-done(((bf16[128,2048]{1,0:T(8,128)(2,1)}), bf16[1024,2048]{1,0:T(8,128)(2,1)}) %all-gather.8.cloned.1.call-update) | async-done | bytes 4194320 | tf_op jit(solution)/shard_map/all_gather | solution.py:110
  478.2 5.9 multiply_convert_fusion
  484.1 2.9 copy.19
  487.0 2.8 reshape.74
  489.8 3.3 copy.20
  493.1 35.0 %while.22 = (s32[]{:T(128)}, f32[64,8,256]{2,1,0:T(8,128)S(1)}, bf16[4,512,64,8]{1,3,2,0:T(8,128)(2,1)}, s32[4,512,64]{1,2,0:T(8,128)S(1)}, s32[]{:T(128)}, /*index=5*/s32[]{:T(128)}) while((s32[]{:T(128)}, f32[64,8,256]{2,1,0:T(8,128)S(1)}, bf16[4,512,64,8]{1,3,2,0:T(8,128)(2,1)}, s32[4,512,64]{1,2,0:T(8,128)S(1)}, s32[]{:T(128)}, ...), condition=%wide.region_13.14_spmd.clone, body=%wide.region_12.13_spmd.clone.sunk | while | flops 142868480 | bytes 1966675 | solution.py:132
  493.1 8.7 %fusion.45 = f32[64,8,256]{2,1,0:T(8,128)S(1)} fusion(s32[512,64]{0,1:T(8,128)S(1)} %dynamic-slice_bitcast_fusion.5, f32[64,8,256]{2,1,0:T(8,128)S(1)} %get-tuple-element.191, bf16[4,512,64,8]{1,3,2,0:T(8,128)(2,1)} %get-tuple-element.198, s32[]{:T(128)} %get-tuple-element.190, pred[]{:T(512)S(6)} %compare.3), kind=kOutput, calls=%fused_computation.10.clone.1 | convolution fusion | flops 142868480 | bytes 1704449 | tf_op jit(solution)/shard_map/while/body/eval_jaxpr/pmk,pmd->mdk/dot_general | solution.py:128
  501.9 8.7 %fusion.45 = f32[64,8,256]{2,1,0:T(8,128)S(1)} fusion(s32[512,64]{0,1:T(8,128)S(1)} %dynamic-slice_bitcast_fusion.5, f32[64,8,256]{2,1,0:T(8,128)S(1)} %get-tuple-element.191, bf16[4,512,64,8]{1,3,2,0:T(8,128)(2,1)} %get-tuple-element.198, s32[]{:T(128)} %get-tuple-element.190, pred[]{:T(512)S(6)} %compare.3), kind=kOutput, calls=%fused_computation.10.clone.1 | convolution fusion | flops 142868480 | bytes 1704449 | tf_op jit(solution)/shard_map/while/body/eval_jaxpr/pmk,pmd->mdk/dot_general | solution.py:128
  510.6 8.7 %fusion.45 = f32[64,8,256]{2,1,0:T(8,128)S(1)} fusion(s32[512,64]{0,1:T(8,128)S(1)} %dynamic-slice_bitcast_fusion.5, f32[64,8,256]{2,1,0:T(8,128)S(1)} %get-tuple-element.191, bf16[4,512,64,8]{1,3,2,0:T(8,128)(2,1)} %get-tuple-element.198, s32[]{:T(128)} %get-tuple-element.190, pred[]{:T(512)S(6)} %compare.3), kind=kOutput, calls=%fused_computation.10.clone.1 | convolution fusion | flops 142868480 | bytes 1704449 | tf_op jit(solution)/shard_map/while/body/eval_jaxpr/pmk,pmd->mdk/dot_general | solution.py:128
  519.4 8.7 %fusion.45 = f32[64,8,256]{2,1,0:T(8,128)S(1)} fusion(s32[512,64]{0,1:T(8,128)S(1)} %dynamic-slice_bitcast_fusion.5, f32[64,8,256]{2,1,0:T(8,128)S(1)} %get-tuple-element.191, bf16[4,512,64,8]{1,3,2,0:T(8,128)(2,1)} %get-tuple-element.198, s32[]{:T(128)} %get-tuple-element.190, pred[]{:T(512)S(6)} %compare.3), kind=kOutput, calls=%fused_computation.10.clone.1 | convolution fusion | flops 142868480 | bytes 1704449 | tf_op jit(solution)/shard_map/while/body/eval_jaxpr/pmk,pmd->mdk/dot_general | solution.py:128
  528.1 0.7 convert_element_type.58
  528.9 6.5 convolution_multiply_fusion.1
  535.4 77.4 %all-reduce.4 = bf16[1024,512]{1,0:T(8,128)(2,1)S(1)} all-reduce(f32[1024,512]{1,0:T(8,128)} %convolution_multiply_fusion.1), channel_id=1, replica_groups=mesh['psg'=16,'qry_0'=4,'qry_1'=2] {'psg'}, use_global_device_ids=true, to_apply=%region_9.10 | all-reduce | flops 524288 | bytes 3145728 | tf_op jit(solution)/shard_map/psum | solution.py:112
  612.8 8.9 %convolution_convert_fusion = bf16[1024,4096]{1,0:T(8,128)(2,1)} fusion(bf16[4096,512]{1,0:T(8,128)(2,1)} %all-gather.6.cloned.1.call-done, bf16[1024,512]{1,0:T(8,128)(2,1)S(1)} %all-reduce.4), kind=kOutput, calls=%fused_computation.20 | convolution fusion | flops 4299161600 | bytes 13631488 | tf_op jit(solution)/shard_map/dot_general | solution.py:141
  621.8 2.4 fusion.20
  624.2 44.1 %all-reduce.3.cloned.1.call-done = bf16[64,8,256]{2,1,0:T(8,128)(2,1)} async-done(((bf16[64,8,256]{2,1,0:T(8,128)(2,1)}), bf16[64,8,256]{2,1,0:T(8,128)(2,1)}) %all-reduce.3.cloned.1.call-update) | async-done | bytes 262160 | tf_op jit(solution)/shard_map/psum | solution.py:135
  668.2 1.8 convert_element_type.59
  670.0 170.9 %reduce-scatter.8.cloned.1.call-done = bf16[128,4096]{1,0:T(8,128)(2,1)} async-done(((bf16[1024,4096]{1,0:T(8,128)(2,1)}), bf16[128,4096]{1,0:T(8,128)(2,1)}) %reduce-scatter.8.cloned.1.call-update) | async-done | bytes 1048592 | tf_op jit(solution)/shard_map/reduce_scatter | solution.py:144
  840.9 1.8 fusion.13
  842.7 2.9 fusion.18
  (63 shorter events, 1.6 us)
Async XLA Ops:
  7.2 173.7 %all-gather.4.cloned.1.call-start = ((), (), s32[]{:S(2)}) async-start(), calls=%async_computation.4 | async-start | bytes 9437184 | tf_op jit(solution)/shard_map/all_gather | solution.py:60
  7.9 231.9 %all-gather.6.cloned.1.call-start = ((), (), s32[]{:S(2)}) async-start(), calls=%async_computation.5 | async-start | bytes 4456448 | tf_op jit(solution)/shard_map/all_gather | solution.py:65
  8.6 325.1 %reduce-scatter.4.cloned.1.call-start = ((), (), s32[]{:S(2)}) async-start(), calls=%async_computation.6 | async-start | bytes 10485760 | tf_op jit(solution)/shard_map/reduce_scatter | solution.py:15
  42.9 143.1 %copy-start.1 = (f32[4096]{0:T(1024)S(1)}, f32[4096]{0:T(1024)}, u32[]{:S(2)}) copy-start(f32[4096]{0:T(1024)} %param.11) | copy-start | bytes 49156
  196.3 53.5 %copy-start.2 = (bf16[4,512,512]{2,1,0:T(8,128)(2,1)S(1)}, bf16[4,512,512]{2,1,0:T(8,128)(2,1)}, u32[]{:S(2)}) copy-start(bf16[4,512,512]{2,1,0:T(8,128)(2,1)} %get-tuple-element.48) | copy-start | bytes 6291460
  248.9 1.0 copy-start.3
  255.5 222.7 %copy-start.4 = (bf16[1024,512]{1,0:T(8,128)(2,1)S(1)}, bf16[1024,512]{1,0:T(8,128)(2,1)}, u32[]{:S(2)}) copy-start(bf16[1024,512]{1,0:T(8,128)(2,1)} %copy-done.3) | copy-start | bytes 3145732
  255.5 114.4 %reduce-scatter.6.cloned.1.call-start = ((), (), s32[]{:S(2)}) async-start(), calls=%async_computation.7 | async-start | bytes 3145728 | tf_op jit(solution)/shard_map/reduce_scatter | solution.py:15
  333.8 144.4 %all-gather.8.cloned.1.call-start = ((), (), s32[]{:S(2)}) async-start(), calls=%async_computation.8 | async-start | bytes 4718592 | tf_op jit(solution)/shard_map/all_gather | solution.py:110
  390.7 277.5 %all-reduce.3.cloned.1.call-start = ((), (), s32[]{:S(2)}) async-start(), calls=%async_computation.10 | async-start | bytes 524288 | tf_op jit(solution)/shard_map/psum | solution.py:135
  528.9 312.1 %reduce-scatter.8.cloned.1.call-start = ((), (), s32[]{:S(2)}) async-start(), calls=%async_computation.9 | async-start | bytes 9437184 | tf_op jit(solution)/shard_map/reduce_scatter | solution.py:144
  621.8 219.2 %copy-start = (bf16[128,4096]{1,0:T(8,128)(2,1)S(1)}, bf16[128,4096]{1,0:T(8,128)(2,1)}, u32[]{:S(2)}) copy-start(bf16[128,4096]{1,0:T(8,128)(2,1)} %param.10) | copy-start | bytes 3145732
Sparse Core Ops, SparseCore 0:
  9.6 171.2 all-gather.3
  183.4 56.3 all-gather.5
  255.6 78.1 reduce-scatter.3
  336.0 33.8 reduce-scatter.5
  390.9 87.2 all-gather.7
  529.0 139.1 all-reduce.2
  670.6 170.2 reduce-scatter.7
where the time goes:
time: 854 us; the launch traced here: 852 us
  waiting for transfers between devices  599 us (70%)
  matrix products  102 us (12%)
  blocking collectives  91.8 us (11%)
  other arithmetic  29.4 us (3%)
  local copies, waits for them, and re-layouts  15.8 us (2%)
  between operations  14.3 us (2%)
    reduce_scatter x1, waiting for transfers between devices, per_device(): lax.psum_scatter(norm_part.astype(jnp.bfloat16), QRY, scatter_dimension=0...  171 us
    all_gather x1, waiting for transfers between devices, per_device(): gathered = lax.all_gather(hidden, QRY, axis=0, tiled=True)  138 us
    reduce_scatter x2, waiting for transfers between devices, summed_rows(): nearer = lax.psum_scatter(x, axes[0], scatter_dimension=dim, tiled=True)  114 us
    all_gather x1, waiting for transfers between devices, per_device(): all_grad = lax.all_gather(score_grad, QRY, axis=0, tiled=True)  87.4 us
    psum x1, blocking collectives, per_device(): query_grad = lax.psum(query_part, 'psg').astype(jnp.bfloat16)  77.4 us
    psum x1, waiting for transfers between devices, per_device(): lax.psum(book_part.astype(jnp.bfloat16), 'psg').astype(jnp.float32)  44.1 us
    all_gather x1, waiting for transfers between devices, per_device(): whole_weight = lax.all_gather(proj_weight, 'psg', axis=0, tiled=True)  43.5 us
    dot_general x4, matrix products, add_book(): jnp.einsum('pmk,pmd->mdk', hot_table, grad_block, preferred_element_type=...  34.9 us
  transfers between devices with their start and end apart: 7, of which 7 were waited for; matrix products, arithmetic and copies ran while one was open for 8% of the time, Pallas kernels for 0%

commit v1 on v0

--- a/solution.py
+++ b/solution.py
@@ -107,7 +107,9 @@
     score_grad = (
         jnp.exp(scores - row_max[:, None]) / row_total[:, None] - target.astype(jnp.float32)
     ).astype(jnp.bfloat16)
-    all_grad = lax.all_gather(score_grad, QRY, axis=0, tiled=True)
+    all_grad = jnp.concatenate(
+        lax.all_to_all(jnp.stack([score_grad] * lax.axis_size(QRY)), QRY, 0, 0), axis=0
+    )
     query_part = jnp.dot(all_grad, passages, preferred_element_type=jnp.float32) * score_scale
     query_grad = lax.psum(query_part, "psg").astype(jnp.bfloat16)
     passage_grad = (

time: 854 us -> 824 us (0.965)
  waiting for transfers between devices: 599 us -> 566 us
    all_gather x1 -> x0, waiting for transfers between devices: 87.4 us -> none  [per_device(): all_grad = lax.all_gather(score_grad, QRY, axis=0, tiled=True)]
    all_to_all x0 -> x1, waiting for transfers between devices: none -> 49.1 us  [per_device(): lax.all_to_all(jnp.stack([score_grad] * lax.axis_size(QRY)), QRY, 0, 0)]
where the time goes in v1:
time: 824 us; the launch traced here: 822 us
  waiting for transfers between devices  566 us (69%)
  matrix products  102 us (12%)
  blocking collectives  88.1 us (11%)
  other arithmetic  28.6 us (3%)
  local copies, waits for them, and re-layouts  18.3 us (2%)
  between operations  14.3 us (2%)
    reduce_scatter x1, waiting for transfers between devices, per_device(): lax.psum_scatter(norm_part.astype(jnp.bfloat16), QRY, scatter_dimension=0...  171 us
    all_gather x1, waiting for transfers between devices, per_device(): gathered = lax.all_gather(hidden, QRY, axis=0, tiled=True)  138 us
    reduce_scatter x2, waiting for transfers between devices, summed_rows(): nearer = lax.psum_scatter(x, axes[0], scatter_dimension=dim, tiled=True)  114 us
    psum x1, blocking collectives, per_device(): query_grad = lax.psum(query_part, 'psg').astype(jnp.bfloat16)  73.7 us
    psum x1, waiting for transfers between devices, per_device(): lax.psum(book_part.astype(jnp.bfloat16), 'psg').astype(jnp.float32)  50 us
    all_to_all x1, waiting for transfers between devices, per_device(): lax.all_to_all(jnp.stack([score_grad] * lax.axis_size(QRY)), QRY, 0, 0)  49.1 us
    all_gather x1, waiting for transfers between devices, per_device(): whole_weight = lax.all_gather(proj_weight, 'psg', axis=0, tiled=True)  43.5 us
    dot_general x4, matrix products, add_book(): jnp.einsum('pmk,pmd->mdk', hot_table, grad_block, preferred_element_type=...  34.9 us
  transfers between devices with their start and end apart: 7, of which 7 were waited for; matrix products, arithmetic and copies ran while one was open for 8% of the time, Pallas kernels for 0%

profile of v1, /device:TPU:1, one launch (start us, length us, event | category | flops | bytes accessed | tf_op | source)
XLA Modules:
  0.0 822.4 jit_solution(16388595712604016938)
XLA Ops:
  7.2 0.7 all-gather.3.cloned.1.call-update
  7.9 0.7 all-gather.5.cloned.1.call-update
  8.7 1.1 copy.27
  9.8 33.1 %while.21 = (s32[]{:T(128)}, bf16[4,512,512]{2,1,0:T(8,128)(2,1)}, s32[4,512,64]{1,2,0:T(8,128)S(1)}, bf16[64,8,256]{2,1,0:T(8,128)(2,1)}, s32[]{:T(128)}) while((s32[]{:T(128)}, bf16[4,512,512]{2,1,0:T(8,128)(2,1)}, s32[4,512,64]{1,2,0:T(8,128)S(1)}, bf16[64,8,256]{2,1,0:T(8,128)(2,1)}, s32[]{:T(128)}) %tuple.72), condition=%wide.region_2.3_spmd, body=%wide.region_1.2_spmd.sunk | while | flops 142868480 | bytes 3277377 | solution.py:81
  9.8 7.2 fusion.43
  17.2 0.8 constant_dynamic-update-slice_fusion.2
  18.1 7.2 fusion.43
  25.5 0.8 constant_dynamic-update-slice_fusion.2
  26.4 7.2 fusion.43
  33.8 0.9 constant_dynamic-update-slice_fusion.2
  34.6 7.2 fusion.43
  42.1 0.8 constant_dynamic-update-slice_fusion.2
  42.9 138.0 %all-gather.3.cloned.1.call-done = bf16[1024,4096]{1,0:T(8,128)(2,1)} async-done(((bf16[128,4096]{1,0:T(8,128)(2,1)}), bf16[1024,4096]{1,0:T(8,128)(2,1)}) %all-gather.3.cloned.1.call-update) | async-done | bytes 8388624 | tf_op jit(solution)/shard_map/all_gather | solution.py:60
  180.9 5.1 fusion.10
  186.0 10.3 %fusion.12 = bf16[1024,4096]{1,0:T(8,128)(2,1)} fusion(bf16[1024,4096]{1,0:T(8,128)(2,1)} %all-gather.3.cloned.1.call-done, f32[4096]{0:T(1024)S(1)} %copy-done.1, f32[1024]{0:T(1024)S(1)} %add_rsqrt_fusion), kind=kLoop, calls=%fused_computation.19 | loop fusion | flops 16777216 | bytes 16797696 | tf_op jit(solution)/shard_map/convert_element_type | solution.py:63
  196.3 43.5 %all-gather.5.cloned.1.call-done = bf16[4096,512]{1,0:T(8,128)(2,1)} async-done(((bf16[256,512]{1,0:T(8,128)(2,1)}), bf16[4096,512]{1,0:T(8,128)(2,1)}) %all-gather.5.cloned.1.call-update) | async-done | bytes 4194320 | tf_op jit(solution)/shard_map/all_gather | solution.py:65
  239.8 9.1 %convolution_convert_fusion.1 = bf16[1024,512]{1,0:T(8,128)(2,1)S(1)} fusion(bf16[1024,4096]{1,0:T(8,128)(2,1)} %fusion.12, bf16[4096,512]{1,0:T(8,128)(2,1)} %all-gather.5.cloned.1.call-done), kind=kOutput, calls=%fused_computation.35 | convolution fusion | flops 4295491584 | bytes 13631488 | tf_op jit(solution)/shard_map/dot_general | solution.py:66
  248.9 1.0 copy-done.3
  249.8 5.6 convolution_multiply_fusion
  255.5 78.3 %reduce-scatter.4.cloned.1.call-done = f32[256,2048]{1,0:T(8,128)} async-done(((f32[1024,2048]{1,0:T(8,128)}), f32[256,2048]{1,0:T(8,128)}) %reduce-scatter.4.cloned.1.call-update) | async-done | bytes 2097168 | tf_op jit(solution)/shard_map/reduce_scatter | solution.py:15
  333.8 0.8 dynamic-slice_subtract_fusion
  334.6 35.3 %reduce-scatter.6.cloned.1.call-done = f32[128,2048]{1,0:T(8,128)} async-done(((f32[256,2048]{1,0:T(8,128)}), f32[128,2048]{1,0:T(8,128)}) %reduce-scatter.6.cloned.1.call-update) | async-done | bytes 1048592 | tf_op jit(solution)/shard_map/reduce_scatter | solution.py:15
  369.9 1.4 reduce_max.9
  371.2 1.6 exponential_reduce_fusion
  372.9 14.4 %all_to_all.10 = f32[16,3,128]{2,1,0:T(4,128)S(1)} all-to-all(f32[16,3,128]{2,1,0:T(4,128)S(1)} %broadcast_in_dim.28), channel_id=1, replica_groups=mesh['psg'=16,'qry_0'=4,'qry_1'=2] {'psg'}, dimensions={0} | all-to-all | bytes 49152 | tf_op jit(solution)/shard_map/all_to_all | solution.py:21
  388.2 1.6 subtract_convert_fusion
  389.9 2.5 stack.2
  392.4 4.6 all-to-all-start.1
  397.0 49.1 %all-to-all-done.1 = bf16[8,128,2048]{2,1,0:T(8,128)(2,1)} async-done(((bf16[8,128,2048]{2,1,0:T(8,128)(2,1)}), bf16[8,128,2048]{2,1,0:T(8,128)(2,1)}, u32[]{:S(2)}, u32[]{:S(2)}) %all-to-all-start.1) | async-done | bytes 4194336 | tf_op jit(solution)/shard_map/all_to_all | solution.py:111
  446.1 6.2 multiply_convert_fusion
  452.3 5.9 convolution_multiply_fusion.1
  458.2 2.9 copy.19
  461.1 2.8 reshape.80
  463.9 3.4 copy.20
  467.3 35.0 %while.22 = (s32[]{:T(128)}, f32[64,8,256]{2,1,0:T(8,128)S(1)}, bf16[4,512,64,8]{1,3,2,0:T(8,128)(2,1)}, s32[4,512,64]{1,2,0:T(8,128)S(1)}, s32[]{:T(128)}, /*index=5*/s32[]{:T(128)}) while((s32[]{:T(128)}, f32[64,8,256]{2,1,0:T(8,128)S(1)}, bf16[4,512,64,8]{1,3,2,0:T(8,128)(2,1)}, s32[4,512,64]{1,2,0:T(8,128)S(1)}, s32[]{:T(128)}, ...), condition=%wide.region_13.14_spmd.clone, body=%wide.region_12.13_spmd.clone.sunk | while | flops 142868480 | bytes 1966675 | solution.py:134
  467.3 8.7 %fusion.45 = f32[64,8,256]{2,1,0:T(8,128)S(1)} fusion(s32[512,64]{0,1:T(8,128)S(1)} %dynamic-slice_bitcast_fusion.5, f32[64,8,256]{2,1,0:T(8,128)S(1)} %get-tuple-element.191, bf16[4,512,64,8]{1,3,2,0:T(8,128)(2,1)} %get-tuple-element.198, s32[]{:T(128)} %get-tuple-element.190, pred[]{:T(512)S(6)} %compare.3), kind=kOutput, calls=%fused_computation.10.clone.1 | convolution fusion | flops 142868480 | bytes 1704449 | tf_op jit(solution)/shard_map/while/body/eval_jaxpr/pmk,pmd->mdk/dot_general | solution.py:130
  476.1 8.7 %fusion.45 = f32[64,8,256]{2,1,0:T(8,128)S(1)} fusion(s32[512,64]{0,1:T(8,128)S(1)} %dynamic-slice_bitcast_fusion.5, f32[64,8,256]{2,1,0:T(8,128)S(1)} %get-tuple-element.191, bf16[4,512,64,8]{1,3,2,0:T(8,128)(2,1)} %get-tuple-element.198, s32[]{:T(128)} %get-tuple-element.190, pred[]{:T(512)S(6)} %compare.3), kind=kOutput, calls=%fused_computation.10.clone.1 | convolution fusion | flops 142868480 | bytes 1704449 | tf_op jit(solution)/shard_map/while/body/eval_jaxpr/pmk,pmd->mdk/dot_general | solution.py:130
  484.9 8.7 %fusion.45 = f32[64,8,256]{2,1,0:T(8,128)S(1)} fusion(s32[512,64]{0,1:T(8,128)S(1)} %dynamic-slice_bitcast_fusion.5, f32[64,8,256]{2,1,0:T(8,128)S(1)} %get-tuple-element.191, bf16[4,512,64,8]{1,3,2,0:T(8,128)(2,1)} %get-tuple-element.198, s32[]{:T(128)} %get-tuple-element.190, pred[]{:T(512)S(6)} %compare.3), kind=kOutput, calls=%fused_computation.10.clone.1 | convolution fusion | flops 142868480 | bytes 1704449 | tf_op jit(solution)/shard_map/while/body/eval_jaxpr/pmk,pmd->mdk/dot_general | solution.py:130
  493.6 8.7 %fusion.45 = f32[64,8,256]{2,1,0:T(8,128)S(1)} fusion(s32[512,64]{0,1:T(8,128)S(1)} %dynamic-slice_bitcast_fusion.5, f32[64,8,256]{2,1,0:T(8,128)S(1)} %get-tuple-element.191, bf16[4,512,64,8]{1,3,2,0:T(8,128)(2,1)} %get-tuple-element.198, s32[]{:T(128)} %get-tuple-element.190, pred[]{:T(512)S(6)} %compare.3), kind=kOutput, calls=%fused_computation.10.clone.1 | convolution fusion | flops 142868480 | bytes 1704449 | tf_op jit(solution)/shard_map/while/body/eval_jaxpr/pmk,pmd->mdk/dot_general | solution.py:130
  502.4 0.7 convert_element_type.58
  503.2 73.7 %all-reduce.4 = bf16[1024,512]{1,0:T(8,128)(2,1)S(1)} all-reduce(f32[1024,512]{1,0:T(8,128)} %convolution_multiply_fusion.1), channel_id=1, replica_groups=mesh['psg'=16,'qry_0'=4,'qry_1'=2] {'psg'}, use_global_device_ids=true, to_apply=%region_9.10 | all-reduce | flops 524288 | bytes 3145728 | tf_op jit(solution)/shard_map/psum | solution.py:114
  576.9 8.9 %convolution_convert_fusion = bf16[1024,4096]{1,0:T(8,128)(2,1)} fusion(bf16[4096,512]{1,0:T(8,128)(2,1)} %all-gather.5.cloned.1.call-done, bf16[1024,512]{1,0:T(8,128)(2,1)S(1)} %all-reduce.4), kind=kOutput, calls=%fused_computation.20 | convolution fusion | flops 4299161600 | bytes 13631488 | tf_op jit(solution)/shard_map/dot_general | solution.py:143
  585.9 2.4 fusion.20
  588.2 50.0 %all-reduce.3.cloned.1.call-done = bf16[64,8,256]{2,1,0:T(8,128)(2,1)} async-done(((bf16[64,8,256]{2,1,0:T(8,128)(2,1)}), bf16[64,8,256]{2,1,0:T(8,128)(2,1)}) %all-reduce.3.cloned.1.call-update) | async-done | bytes 262160 | tf_op jit(solution)/shard_map/psum | solution.py:137
  638.3 1.8 convert_element_type.59
  640.1 170.8 %reduce-scatter.8.cloned.1.call-done = bf16[128,4096]{1,0:T(8,128)(2,1)} async-done(((bf16[1024,4096]{1,0:T(8,128)(2,1)}), bf16[128,4096]{1,0:T(8,128)(2,1)}) %reduce-scatter.8.cloned.1.call-update) | async-done | bytes 1048592 | tf_op jit(solution)/shard_map/reduce_scatter | solution.py:146
  810.9 1.8 fusion.13
  812.7 2.9 fusion.18
  (61 shorter events, 2.3 us)
Async XLA Ops:
  7.2 173.7 %all-gather.3.cloned.1.call-start = ((), (), s32[]{:S(2)}) async-start(), calls=%async_computation.5 | async-start | bytes 9437184 | tf_op jit(solution)/shard_map/all_gather | solution.py:60
  7.9 231.9 %all-gather.5.cloned.1.call-start = ((), (), s32[]{:S(2)}) async-start(), calls=%async_computation.6 | async-start | bytes 4456448 | tf_op jit(solution)/shard_map/all_gather | solution.py:65
  8.6 325.1 %reduce-scatter.4.cloned.1.call-start = ((), (), s32[]{:S(2)}) async-start(), calls=%async_computation.7 | async-start | bytes 10485760 | tf_op jit(solution)/shard_map/reduce_scatter | solution.py:15
  42.9 143.1 %copy-start.1 = (f32[4096]{0:T(1024)S(1)}, f32[4096]{0:T(1024)}, u32[]{:S(2)}) copy-start(f32[4096]{0:T(1024)} %param.11) | copy-start | bytes 49156
  196.3 53.5 %copy-start.2 = (bf16[4,512,512]{2,1,0:T(8,128)(2,1)S(1)}, bf16[4,512,512]{2,1,0:T(8,128)(2,1)}, u32[]{:S(2)}) copy-start(bf16[4,512,512]{2,1,0:T(8,128)(2,1)} %get-tuple-element.48) | copy-start | bytes 6291460
  248.9 1.0 copy-start.3
  255.4 114.4 %reduce-scatter.6.cloned.1.call-start = ((), (), s32[]{:S(2)}) async-start(), calls=%async_computation.8 | async-start | bytes 3145728 | tf_op jit(solution)/shard_map/reduce_scatter | solution.py:15
  392.4 53.8 %all-to-all-start.1 = ((bf16[8,128,2048]{2,1,0:T(8,128)(2,1)}), bf16[8,128,2048]{2,1,0:T(8,128)(2,1)}, u32[]{:S(2)}, u32[]{:S(2)}) async-start(bf16[8,128,2048]{2,1,0:T(8,128)(2,1)} %stack.2), calls=%async_computation.3 | async-start | bytes 8388608 | tf_op jit(solution)/shard_map/all_to_all | solution.py:111
  397.0 241.3 %all-reduce.3.cloned.1.call-start = ((), (), s32[]{:S(2)}) async-start(), calls=%async_computation.10 | async-start | bytes 524288 | tf_op jit(solution)/shard_map/psum | solution.py:137
  503.1 307.7 %reduce-scatter.8.cloned.1.call-start = ((), (), s32[]{:S(2)}) async-start(), calls=%async_computation.9 | async-start | bytes 9437184 | tf_op jit(solution)/shard_map/reduce_scatter | solution.py:146
  585.8 225.0 %copy-start = (bf16[128,4096]{1,0:T(8,128)(2,1)S(1)}, bf16[128,4096]{1,0:T(8,128)(2,1)}, u32[]{:S(2)}) copy-start(bf16[128,4096]{1,0:T(8,128)(2,1)} %param.10) | copy-start | bytes 3145732
Sparse Core Ops, SparseCore 0:
  9.6 171.2 all-gather.2
  183.4 56.3 all-gather.4
  255.6 78.1 reduce-scatter.3
  336.0 33.8 reduce-scatter.5
  503.2 135.0 all-reduce.2
  640.5 170.2 reduce-scatter.7
